TPU v7x, 32 devices: a whole 2x2x4 slice. The times are simulated.
32 devices in a mesh: section: 4 (over y, x), stem: 8 (over z, core).
Axes of the slice: x: 2, y: 2, z: 4, core: 2. Of those that a mesh axis runs over, the one named last changes fastest.
Arguments:
- bitstrings: int32 [4, 4, 32, 3], P('section'), may hold values 0 or 1
- boundary: float32 [2, 2048], replicated, may hold values from -6 to 6
- stem_tensor: float32 [4, 2, 2048, 8, 2048], P('section', None, 'stem'), may hold values from -0.09375 to 0.09375
- probe_vectors: float32 [4, 2, 2048], P('section'), may hold values from -0.09375 to 0.09375
- inbound_permutations: int32 [4, 2048], replicated, may hold values from 0 to 2047, each once within a row
Outputs:
- amplitudes: float32 [4, 2, 4, 32], P('section')
Inputs may be any that keep to these rules, and one draw needn't show every extreme that they name: `inbound_permutations`: each row of relabeling names every number of 0 to 2047 once.
All inputs are finite; a program needn't handle non-finite values. No bound on the sum of `bitstrings` on one device may be relied on, other than what follows from the above.
Results may differ from a plain program's by a relative error of at most 0.0003.
Values sent between devices are 32-bit elements; how exact they have to be, the bound alone decides.
A program may use at most 128 MiB of HBM per device.

v0:
```python
import functools

import jax
import jax.numpy as jnp
from jax import lax
from jax.experimental import pallas as pl
from jax.experimental.pallas import tpu as pltpu
from jax.sharding import PartitionSpec as P

HIGH = lax.Precision.HIGH
HIGHEST = lax.Precision.HIGHEST


def halves(x):
    hi = lax.reduce_precision(x, 8, 7)
    return hi.astype(jnp.bfloat16), (x - hi).astype(jnp.bfloat16)


def select_columns(x, chosen):
    rows = x.shape[0]
    pick = (jnp.arange(x.shape[1], dtype=jnp.int32)[:, None] == chosen[None, :]).astype(jnp.bfloat16)
    hi, lo = halves(x)
    both = jnp.dot(jnp.concatenate([hi, lo]), pick, preferred_element_type=jnp.float32)
    return both[:rows] + both[rows:]


MESH = pl.DeviceIdType.MESH
VMEM = pl.BlockSpec(memory_space=pltpu.VMEM)


def send(src, dst, send_sem, recv_sem, target):
    return pltpu.make_async_remote_copy(
        src_ref=src, dst_ref=dst, send_sem=send_sem, recv_sem=recv_sem, device_id=target, device_id_type=MESH
    )


def greet(targets):
    barrier = pltpu.get_barrier_semaphore()
    for target in targets:
        pl.semaphore_signal(barrier, inc=1, device_id=target, device_id_type=MESH)
    pl.semaphore_wait(barrier, len(targets))


def call(kernel, outs, scratch, collective_id, *args):
    return pl.pallas_call(
        kernel,
        out_shape=[jax.ShapeDtypeStruct(shape, jnp.float32) for shape in outs],
        in_specs=[VMEM] * len(args),
        out_specs=[VMEM] * len(outs),
        scratch_shapes=scratch,
        compiler_params=pltpu.CompilerParams(collective_id=collective_id, has_side_effects=True),
    )(*args)


def exchange_kernel(S, R, v_ref, set_ref, out_ref, sets_ref, land, total, s1, r1, s2, r2, s3, r3):
    me_s, me_r = lax.axis_index("section"), lax.axis_index("stem")
    partner = me_s + 1 - 2 * (me_s % 2)
    ranks = [(me_r + d) % R for d in range(R)]
    others = [(me_s + d) % S for d in range(S)]
    greet(
        [(me_s, r) for r in ranks[1:]] + [(partner, r) for r in ranks] + [(s, me_r) for s in others[1:]]
    )
    first = [
        send(v_ref.at[ranks[d]], land.at[d - 1], s1.at[d - 1], r1.at[d - 1], (me_s, ranks[d])) for d in range(1, R)
    ]
    third = [
        send(set_ref, sets_ref.at[me_s], s3.at[d - 1], r3.at[d - 1], (others[d], me_r)) for d in range(1, S)
    ]
    for copy in first + third:
        copy.start()
    sets_ref[me_s] = set_ref[...]
    value = v_ref[me_r]
    for d in range(1, R):
        first[d - 1].wait_recv()
        value = value + land[d - 1]
    total[...] = value
    second = [send(total, out_ref.at[me_r], s2.at[d], r2.at[d], (partner, ranks[d])) for d in range(R)]
    for copy in second:
        copy.start()
    for copy in first:
        copy.wait_send()
    for copy in second + third:
        copy.wait()


def exchange(S, R, v, sets):
    return call(
        functools.partial(exchange_kernel, S, R),
        [v.shape, (S,) + sets.shape],
        [
            pltpu.VMEM((R - 1,) + v.shape[1:], jnp.float32),
            pltpu.VMEM(v.shape[1:], jnp.float32),
            pltpu.SemaphoreType.DMA((R - 1,)),
            pltpu.SemaphoreType.DMA((R - 1,)),
            pltpu.SemaphoreType.DMA((R,)),
            pltpu.SemaphoreType.DMA((R,)),
            pltpu.SemaphoreType.DMA((S - 1,)),
            pltpu.SemaphoreType.DMA((S - 1,)),
        ],
        1,
        v,
        sets,
    )


def meet_kernel(
    S, R, u_ref, w_ref, f_ref, g_ref, h_ref, e_ref, sum_ref, land, out_ref, su, ru, sw, rw,
    part, land1, half, far, s1, r1, s2, r2,
):
    me_s, me_r = lax.axis_index("section"), lax.axis_index("stem")
    ranks = [(me_r + d) % R for d in range(R)]
    greet([((me_s + e) % S, ranks[d]) for e in range(S) for d in range(R) if e + d])
    def u_copies():
        return [
            send(u_ref.at[ranks[d] * S + s], land.at[me_r], su.at[d * S + s], ru.at[me_r], (s, ranks[d]))
            for d in range(R)
            for s in range(S)
            if s != 1 or d
        ]

    def w_copies():
        return [send(w_ref.at[s], out_ref, sw.at[s], rw.at[0], (s, me_r)) for s in range(S) if s != 2]

    def arrived(rank):
        send(land.at[rank], land.at[rank], su.at[0], ru.at[rank], (me_s, ranks[1])).wait_recv()

    @pl.when(me_s == 1)
    def _():
        for copy in u_copies():
            copy.start()
        land[me_r] = u_ref[me_r * S + 1]

    @pl.when(me_s == 2)
    def _():
        for copy in w_copies():
            copy.start()
        out_ref[...] = w_ref[2]

    @pl.when(me_s == 1)
    def _():
        for d in range(1, R):
            arrived(ranks[d])
        for copy in u_copies():
            copy.wait_send()

    @pl.when(me_s != 1)
    def _():
        for rank in range(R):
            arrived(rank)

    @pl.when(me_s == 2)
    def _():
        for copy in w_copies():
            copy.wait_send()

    @pl.when(me_s != 2)
    def _():
        send(out_ref, out_ref, sw.at[0], rw.at[0], (me_s, ranks[1])).wait_recv()

    value = land[0]
    for rank in range(1, R):
        value = value + land[rank]

    def dot(a, b):
        return jnp.dot(a, b, precision=HIGHEST, preferred_element_type=jnp.float32)

    def put(row, a, b):
        n = a.shape[1] // 2
        part[row : row + 1, :] = jnp.sum(a[:, :n] * b[:, :n] - a[:, n:] * b[:, n:], axis=0, keepdims=True)
        part[row + 1 : row + 2, :] = jnp.sum(a[:, :n] * b[:, n:] + a[:, n:] * b[:, :n], axis=0, keepdims=True)

    front = dot(value, f_ref[...])
    wide = out_ref.shape[1] // 2
    part[0:4, :] = e_ref[0:4, :]
    put(4, front, dot(out_ref[:, wide:], h_ref[...]))
    put(6, front, dot(out_ref[:, :wide], g_ref[...]))

    near = [(me_s, ranks[d]) for d in range(1, R)]
    across = [((me_s + d) % S, me_r) for d in range(1, S)]
    first = [send(part, land1.at[d], s1.at[d], r1.at[d], near[d]) for d in range(R - 1)]
    for copy in first:
        copy.start()
    value = part[...]
    for d in range(R - 1):
        first[d].wait_recv()
        value = value + land1[d]
    half[...] = value
    second = [send(half, far.at[d], s2.at[d], r2.at[d], across[d]) for d in range(S - 1)]
    for copy in second:
        copy.start()
    for d in range(S - 1):
        second[d].wait_recv()
        value = value + far[d]
    sum_ref[...] = value
    for copy in first + second:
        copy.wait_send()


def meet(S, R, u, w, f, g, h, e):
    return call(
        functools.partial(meet_kernel, S, R),
        [e.shape],
        [
            pltpu.VMEM((R,) + u.shape[1:], jnp.float32),
            pltpu.VMEM(w.shape[1:], jnp.float32),
            pltpu.SemaphoreType.DMA((S * R,)),
            pltpu.SemaphoreType.DMA((R,)),
            pltpu.SemaphoreType.DMA((S,)),
            pltpu.SemaphoreType.DMA((1,)),
            pltpu.VMEM(e.shape, jnp.float32),
            pltpu.VMEM((R - 1,) + e.shape, jnp.float32),
            pltpu.VMEM(e.shape, jnp.float32),
            pltpu.VMEM((S - 1,) + e.shape, jnp.float32),
            pltpu.SemaphoreType.DMA((R - 1,)),
            pltpu.SemaphoreType.DMA((R - 1,)),
            pltpu.SemaphoreType.DMA((S - 1,)),
            pltpu.SemaphoreType.DMA((S - 1,)),
        ],
        2,
        u,
        w,
        f,
        g,
        h,
        e,
    )[0]


def local(bitstrings, boundary, stem_tensor, probe_vectors, inbound_permutations):
    section = lax.axis_index("section")
    sections = lax.axis_size("section")
    rank = lax.axis_index("stem")
    rows, settings, width = stem_tensor.shape[2:]
    bonds = boundary.shape[1]
    micro, batch, qubits = bitstrings.shape[1:]
    count = micro * batch
    powers = jnp.left_shift(jnp.int32(1), jnp.arange(qubits, dtype=jnp.int32))
    own_setting = jnp.sum(bitstrings[0] * powers, axis=-1).reshape(count)
    ranks = lax.axis_size("stem")
    probe = probe_vectors[0]
    perm = inbound_permutations

    def flat(plane):
        return stem_tensor[0, plane].reshape(rows * settings, width)

    def own_rows(row):
        return lax.dynamic_slice_in_dim(row, rank * rows, rows)

    zeros_a = jnp.zeros((2 * settings, bonds), jnp.float32)

    def first_forward():
        t_re, t_im = stem_tensor[0, 0], stem_tensor[0, 1]
        b = jnp.dot(
            boundary,
            (jnp.arange(bonds, dtype=jnp.int32)[:, None] == own_rows(perm[0])[None, :]).astype(jnp.float32),
            precision=HIGHEST,
        )
        b_re, b_im = b[0][:, None, None], b[1][:, None, None]
        u_re = jnp.sum(b_re * t_re - b_im * t_im, axis=0)
        u_im = jnp.sum(b_re * t_im + b_im * t_re, axis=0)
        return jnp.concatenate([u_re, u_im])

    def last_backward():
        t_re, t_im = stem_tensor[0, 0], stem_tensor[0, 1]
        v_re = jnp.sum(t_re * probe[0] - t_im * probe[1], axis=-1)
        v_im = jnp.sum(t_re * probe[1] + t_im * probe[0], axis=-1)
        v = jnp.concatenate([v_re.T, v_im.T])
        return lax.dynamic_update_slice_in_dim(zeros_a, v, rank * rows, 1)

    idle = lambda: zeros_a
    vectors = lax.switch(section, [first_forward, idle, idle, last_backward])

    own_vectors = vectors
    blocks = vectors.reshape(2 * settings, ranks, rows).transpose(1, 0, 2)
    own_block = jnp.broadcast_to(own_setting.astype(jnp.float32), (8, count))
    blocks, setting = exchange(sections, ranks, blocks, own_block)
    setting = setting[:, 0].astype(jnp.int32)
    vectors = blocks.transpose(1, 0, 2).reshape(2 * settings, bonds)

    ends = settings + 1
    pairs = settings * settings
    zeros_u = jnp.zeros((bonds, 2 * pairs), jnp.float32)
    zeros_w = jnp.zeros((rows, 4 * pairs), jnp.float32)
    zeros_p = jnp.zeros((2, count), jnp.float32)

    def onehot(ids, size):
        return (jnp.arange(size, dtype=jnp.int32)[:, None] == ids[None, :]).astype(jnp.float32)

    def twice(pick):
        return jnp.kron(jnp.eye(2, dtype=jnp.float32), pick)

    front = onehot(setting[0] * settings + setting[1], pairs)

    def with_probe(v, pick):
        m = lax.dot_general(v, probe, (((1,), (1,)), ((), ())), precision=HIGHEST)
        n = m.shape[0] // 2
        amp = jnp.stack([m[:n, 0] - m[n:, 1], m[:n, 1] + m[n:, 0]])
        return jnp.dot(amp, pick, precision=HIGHEST)

    def first_amplitudes():
        return zeros_u, zeros_w, with_probe(own_vectors, onehot(setting[0], settings))

    def second_forward():
        x = select_columns(vectors, jnp.repeat(own_rows(perm[1]), settings))
        same = jnp.arange(rows * settings, dtype=jnp.int32)[None, :] % settings
        same = (same == jnp.arange(settings, dtype=jnp.int32)[:, None]).astype(jnp.float32)
        spread = (x[:, None, :] * same[None]).reshape(2 * pairs, rows * settings)
        p_re = jnp.dot(spread, flat(0), precision=HIGH)
        p_im = jnp.dot(spread, flat(1), precision=HIGH)
        u_re = p_re[:pairs] - p_im[pairs:]
        u_im = p_im[:pairs] + p_re[pairs:]
        u = jnp.concatenate([u_re, u_im])
        amp = with_probe(u, front)
        hi, lo = halves(u)
        pick = (perm[2][:, None] == jnp.arange(bonds, dtype=jnp.int32)[None, :]).astype(jnp.bfloat16)
        both = lax.dot_general(
            pick, jnp.concatenate([hi, lo]), (((1,), (1,)), ((), ())), preferred_element_type=jnp.float32
        )
        return both[:, : 2 * pairs] + both[:, 2 * pairs :], zeros_w, amp

    def second_backward():
        place = (perm[3][:, None] == jnp.arange(bonds, dtype=jnp.int32)[None, :]).astype(jnp.bfloat16)
        hi, lo = halves(vectors)
        both = jnp.dot(jnp.concatenate([hi, lo]), place, preferred_element_type=jnp.float32)
        v = (both[: 2 * settings] + both[2 * settings :]).reshape(2, settings, bonds)
        v = jnp.concatenate([v, probe[:, None, :]], axis=1).reshape(2 * ends, bonds)
        q_re = lax.dot_general(flat(0), v, (((1,), (1,)), ((), ())), precision=HIGH)
        q_im = lax.dot_general(flat(1), v, (((1,), (1,)), ((), ())), precision=HIGH)
        w_re = q_re[:, :ends] - q_im[:, ends:]
        w_im = q_re[:, ends:] + q_im[:, :ends]
        w_re, w_im = w_re.reshape(rows, settings, ends), w_im.reshape(rows, settings, ends)
        w = jnp.concatenate(
            [
                w_re[:, :, :settings].reshape(rows, pairs),
                w_im[:, :, :settings].reshape(rows, pairs),
                w_re[:, :, settings],
                w_im[:, :, settings],
                jnp.zeros((rows, 2 * pairs - 2 * settings), jnp.float32),
            ],
            axis=1,
        )
        return zeros_u, w, zeros_p

    none = lambda: (zeros_u, zeros_w, zeros_p)
    u, w, amp = lax.switch(section, [first_amplitudes, second_forward, second_backward, none])
    share = rows // sections
    unused = jnp.zeros((2 * (pairs - settings), 2 * count), jnp.float32)
    nothing = jnp.zeros_like(amp)
    summed = meet(
        sections,
        ranks,
        u.reshape(sections * ranks, share, 2 * pairs),
        w.reshape(sections, share, 4 * pairs),
        twice(front),
        twice(onehot(setting[2] * settings + setting[3], pairs)),
        jnp.concatenate([twice(onehot(setting[2], settings)), unused]),
        jnp.concatenate(
            [jnp.where(section == 0, amp, 0.0), jnp.where(section == 1, amp, 0.0), nothing, nothing]
        ),
    ).reshape(sections, 2, count)
    own = lax.dynamic_index_in_dim(summed, section, 0, False)
    return own.reshape(1, 2, micro, batch)


def solution(mesh):
    return jax.shard_map(
        local,
        mesh=mesh,
        in_specs=(
            P("section", None, None, None),
            P(),
            P("section", None, "stem", None, None),
            P("section", None, None),
            P(),
        ),
        out_specs=P("section", None, None, None),
        check_vma=False,
    )
```

profile of v0, /device:TPU:0, one launch (start us, length us, event | category | flops | bytes accessed | tf_op | source)
XLA Modules:
  0.0 105.4 jit_solution(3779172846378041691)
XLA Ops:
  0.1 0.8 fusion.76
  1.0 0.6 broadcast_in_dim.43.set_ref
  1.6 15.1 %conditional.2 = (f32[16,2048]{1,0:T(8,128)}) conditional(s32[]{:T(128)} %clamp.4, (s32[4,2048]{1,0:T(4,128)}, s32[]{:T(128)}, f32[2,2048]{1,0:T(2,128)}, f32[1,2,256,8,2048]{4,3,2,1,0:T(8,128)}) %tuple.41, () %tuple.42, () %tuple.43, (f32[1,2,256,8,2048]{4,3,2,1,0:T(8,128)}, f32[2,2048]{1,0:T(2,128)}, ...), branch_computations={%region_0.3_spmd, %region_3.4_spmd, %region_4.0_spmd, %region_5.8_... | conditional | flops 46661636 | bytes 33991736 | solution.py:271
  1.6 0.8 slice.103
  2.3 1.4 %fusion.5 = f32[2,256]{1,0:T(2,128)S(1)} fusion(f32[2,2048]{1,0:T(2,128)} %get-tuple-element.83, s32[256]{0:T(256)S(1)} %bitcast.165), kind=kOutput, calls=%fused_computation.10 | convolution fusion | flops 13107200 | bytes 19456 | tf_op jit(solution)/shard_map/cond/branch_0_fun/dot_general | solution.py:253
  3.8 12.2 %fusion.1 = (f32[8,2048]{1,0:T(8,128)S(1)}, f32[8,2048]{1,0:T(8,128)S(1)}) fusion(f32[1,2,256,8,2048]{4,3,2,1,0:T(8,128)} %get-tuple-element.55, f32[256]{0:T(256)S(1)} %bitcast.164, f32[256]{0:T(256)S(1)} %bitcast.163), kind=kLoop, calls=%fused_computation.3 | loop fusion | flops 33521664 | bytes 33687552 | tf_op jit(solution)/shard_map/cond/branch_0_fun/reduce_sum | solution.py:259
  16.0 0.7 pad_maximum_fusion
  16.7 1.6 %copy.45 = f32[2,8,8,256]{3,2,0,1:T(8,128)} copy(f32[2,8,8,256]{3,2,1,0:T(8,128)} %bitcast.45) | data formatting | bytes 262144 | tf_op jit(solution)/shard_map/reshape | solution.py:274
  18.2 16.6 %shard_map.56 = (f32[8,16,256]{2,1,0:T(8,128)}, f32[4,8,128]{2,1,0:T(8,128)}) custom-call(f32[8,16,256]{2,1,0:T(8,128)} %bitcast.149, f32[8,128]{1,0:T(8,128)} %broadcast_in_dim.43.set_ref), custom_call_target="tpu_custom_call" | custom-call | tf_op jit(solution)/shard_map/pallas_call | solution.py:45
  34.8 0.7 slice_convert_fusion
  35.5 0.9 copy.35
  36.5 0.7 concatenate.44.h_ref
  37.2 0.1 broadcast_multiply_fusion
  37.3 0.7 copy.43
  38.0 0.7 copy.44
  38.7 1.8 %conditional.3 = (f32[2,128]{1,0:T(2,128)S(1)}, f32[32,64,128]{2,1,0:T(8,128)S(1)}, f32[4,64,256]{2,1,0:T(8,128)S(1)}) conditional(s32[]{:T(128)} %clamp.4, (f32[16,2048]{1,0:T(8,128)}, f32[2,2048]{1,0:T(2,128)}, s32[4,1,128]{2,1,0:T(1,128)S(1)}) %tuple.81, (f32[16,2048]{1,0:T(8,128)S(1)}, s32[4,2048]{1,0:T(4,128)}, ...), branch_computations={%region_9.0_spmd, %region_10.11_spmd, %region_11.12_spmd, %region_... | conditional | flops 8878436352 | bytes 50216044 | solution.py:345
  38.7 1.1 %fusion.83 = f32[16,2]{0,1:T(2,128)S(1)} fusion(f32[16,2048]{1,0:T(8,128)} %get-tuple-element.59, f32[2,2048]{1,0:T(2,128)} %get-tuple-element.60), kind=kOutput, calls=%fused_computation.142 | convolution fusion | flops 786432 | bytes 147584 | tf_op jit(solution)/shard_map/cond/branch_0_fun/dot_general | solution.py:295
  39.8 0.1 subtract_bitcast_fusion
  39.9 0.2 fusion.11
  40.1 0.1 reshape.282
  40.5 0.7 maximum_maximum_fusion.e_ref
  41.1 63.0 %shard_map.57 = f32[8,128]{1,0:T(8,128)} custom-call(f32[32,64,128]{2,1,0:T(8,128)S(1)} %get-tuple-element.79.u_ref, f32[4,64,256]{2,1,0:T(8,128)S(1)} %get-tuple-element.80.w_ref, f32[128,256]{1,0:T(8,128)} %bitcast.151, f32[128,256]{1,0:T(8,128)} %bitcast.150, f32[128,256]{1,0:T(8,128)} %concatenate.44.h_ref, f32[8,128]{1,0:T(8,128)} %maximum_maximum_fusion.e_ref), custom_call_target="tpu_custom_call" | custom-call | tf_op jit(solution)/shard_map/pallas_call | solution.py:45
  104.1 0.6 constant_dynamic-slice_fusion.2
  104.8 0.7 reshape.300
  (15 shorter events, 0.3 us)
where the time goes:
time: 106 us; the launch traced here: 105 us
  Pallas kernels  79.6 us (75%)
  other arithmetic  15.4 us (15%)
  local copies, waits for them, and re-layouts  7.46 us (7%)
  matrix products  2.73 us (3%)
    pallas_call x2, Pallas kernels, call(): pl.pallas_call(kernel, out_shape=[jax.ShapeDtypeStruct(shape, jnp.float32...  79.6 us
    reduce_sum x1, other arithmetic, first_forward(): u_re = jnp.sum(b_re * t_re - b_im * t_im, axis=0)  12.2 us

commit v1 on v0

v1 whole, which is shorter than its diff:
```python
import functools

import jax
import jax.numpy as jnp
from jax import lax
from jax.experimental import pallas as pl
from jax.experimental.pallas import tpu as pltpu
from jax.sharding import PartitionSpec as P

MESH = pl.DeviceIdType.MESH
VMEM = pl.BlockSpec(memory_space=pltpu.VMEM)
SMEM = pl.BlockSpec(memory_space=pltpu.SMEM)
ANY = pl.BlockSpec(memory_space=pl.ANY)
F32, BF16 = jnp.float32, jnp.bfloat16
LANES = 128
SLOTS = 4
STEP = 16
GROUPS = 4


def send(src, dst, send_sem, recv_sem, target):
    return pltpu.make_async_remote_copy(
        src_ref=src, dst_ref=dst, send_sem=send_sem, recv_sem=recv_sem, device_id=target, device_id_type=MESH
    )


def nn(a, b):
    return jnp.dot(a, b, preferred_element_type=F32)


def nt(a, b):
    return lax.dot_general(a, b, (((1,), (1,)), ((), ())), preferred_element_type=F32)


def halves(x):
    hi = x.astype(BF16)
    return hi, (x - hi.astype(F32)).astype(BF16)


def stacked(x):
    return jnp.concatenate(halves(x), axis=0)


def folded(y):
    n = y.shape[0] // 2
    return y[:n] + y[n:]


def turned(x):
    n = x.shape[0] // 2
    return jnp.concatenate([-x[n:], x[:n]], axis=0)


def rows_of(shape):
    return lax.broadcasted_iota(jnp.int32, shape, 0)


def lanes_of(shape):
    return lax.broadcasted_iota(jnp.int32, shape, 1)


def kernel(
    S, R, rows, P_, K, count,
    bits_ref, bnd_ref, perm0_ref, perm_ref, probe_ref, stem_ref, out_ref,
    buf, hl, place, wide, own, sets, set_own, uland, vland, snd, big, bighl, mine, other, xland, wown, wland, v2land,
    gram, part, fin, total,
    load_sem, set_s, set_r, u_s, u_r, v_s, v_r, v2_s, v2_r, x_s, x_r, w_s, w_r, f_s, f_r,
):
    me_s, me_r = lax.axis_index("section"), lax.axis_index("stem")
    half = R // 2
    parity = me_r % 2
    partner = me_r + 1 - 2 * parity
    chunks = rows // STEP
    C2 = 2 * P_
    tiles = K // LANES

    def load(i):
        slot = i % SLOTS
        for j in range(tiles):
            pltpu.make_async_copy(
                stem_ref.at[:, pl.ds(i * STEP * P_, STEP * P_), pl.ds(j * LANES, LANES)],
                buf.at[slot, j],
                load_sem.at[slot],
            ).start()

    def loaded(slot):
        pltpu.make_async_copy(buf.at[slot], buf.at[slot], load_sem.at[slot]).wait()

    for i in range(min(SLOTS, chunks)):
        load(i)

    barrier = pltpu.get_barrier_semaphore()
    for e in range(S):
        for d in range(R):
            if e + d:
                pl.semaphore_signal(
                    barrier, inc=1, device_id=((me_s + e) % S, (me_r + d) % R), device_id_type=MESH
                )

    qubits, micro, batch = bits_ref.shape
    codes = bits_ref[0].astype(F32)
    for q in range(1, qubits):
        codes = codes + float(2**q) * bits_ref[q].astype(F32)
    spread = jnp.zeros((8, count), F32)
    for m in range(micro):
        shift = (lanes_of((batch, count)) == rows_of((batch, count)) + m * batch).astype(F32).astype(BF16)
        spread = spread + nn(jnp.broadcast_to(codes[m : m + 1, :], (8, batch)).astype(BF16), shift)
    set_own[...] = spread

    own[...] = jnp.zeros_like(own)
    wide[...] = jnp.zeros_like(wide)

    blocks = tiles // chunks

    def build(i):
        for b in range(blocks):
            start = pl.multiple_of((i * blocks + b) * LANES, LANES)
            every = perm_ref[:, pl.ds(start, LANES)].astype(F32)
            row = jnp.sum(jnp.where(rows_of((S, LANES)) == (me_s + 1) % S, every, 0.0), axis=0, keepdims=True)
            col = jnp.broadcast_to(row, (LANES, LANES)).T
            for j in range(tiles):
                target = (lanes_of((LANES, LANES)) + j * LANES).astype(F32)
                place[pl.ds(start, LANES), j * LANES : (j + 1) * LANES] = (col == target).astype(F32).astype(BF16)

    def first(i, slot):
        scal = []
        for k in range(STEP):
            at = perm0_ref[0, me_r * rows + i * STEP + k]
            scal.append((bnd_ref[0, at], bnd_ref[1, at]))
        span = 4
        for g in range(tiles // span):
            cols = [slice((g * span + t) * LANES, (g * span + t + 1) * LANES) for t in range(span)]
            a = [wide[0:P_, js] for js in cols]
            b = [wide[P_:C2, js] for js in cols]
            for k in range(STEP):
                br, bi = scal[k]
                for t in range(span):
                    tr = buf[slot, g * span + t, 0, k * P_ : (k + 1) * P_, :]
                    ti = buf[slot, g * span + t, 1, k * P_ : (k + 1) * P_, :]
                    a[t] = a[t] + (br * tr - bi * ti)
                    b[t] = b[t] + (br * ti + bi * tr)
            for t in range(span):
                wide[0:P_, cols[t]] = a[t]
                wide[P_:C2, cols[t]] = b[t]

    def against_probe(i, slot):
        width = min(rows, LANES)
        block = pl.multiple_of((i * STEP // width) * width, width)
        lane = lanes_of((P_, width))
        at = pl.ds(block, width) if rows > width else slice(None)
        a, b = own[0:P_, at], own[P_:C2, at]
        for k in range(STEP):
            ar = jnp.zeros((P_, LANES), F32)
            ai = jnp.zeros((P_, LANES), F32)
            for j in range(tiles):
                js = slice(j * LANES, (j + 1) * LANES)
                tr = buf[slot, j, 0, k * P_ : (k + 1) * P_, :]
                ti = buf[slot, j, 1, k * P_ : (k + 1) * P_, :]
                pr, pi = wide[0:P_, js], wide[P_:C2, js]
                ar = ar + (tr * pr - ti * pi)
                ai = ai + (tr * pi + ti * pr)
            hit = lane == (i * STEP + k - block)
            a = jnp.where(hit, jnp.sum(ar, axis=1, keepdims=True), a)
            b = jnp.where(hit, jnp.sum(ai, axis=1, keepdims=True), b)
        own[0:P_, at] = a
        own[P_:C2, at] = b

    def split(i, slot):
        at = pl.ds(pl.multiple_of(i * STEP, STEP), STEP)

        def column(j, carry):
            js = pl.ds(pl.multiple_of(j * LANES, LANES), LANES)
            for c in range(2):
                for p in range(P_):
                    hi, lo = halves(buf[slot, j, c, pl.ds(p, STEP, P_), :])
                    hl[c, 0, p, at, js] = hi
                    hl[c, 1, p, at, js] = lo
            return carry

        lax.fori_loop(0, tiles, column, 0)

    @pl.when(me_s >= 2)
    def _():
        wide[0:P_, :] = jnp.broadcast_to(probe_ref[0:1, :], (P_, K))
        wide[P_:C2, :] = jnp.broadcast_to(probe_ref[1:2, :], (P_, K))

    def stream(i, carry):
        slot = i % SLOTS
        loaded(slot)

        @pl.when(me_s == 0)
        def _():
            build(i)
            first(i, slot)

        @pl.when(me_s == 1)
        def _():
            build(i)
            split(i, slot)

        @pl.when(me_s == 2)
        def _():
            build(i)
            split(i, slot)
            against_probe(i, slot)

        @pl.when(me_s == 3)
        def _():
            against_probe(i, slot)

        @pl.when(i + SLOTS < chunks)
        def _():
            load(i + SLOTS)

        return carry

    lax.fori_loop(0, chunks, stream, 0)
    pl.semaphore_wait(barrier, S * R - 1)

    def set_copy():
        return send(set_own, sets.at[me_s], set_s.at[0], set_r.at[me_s], (1, me_r))

    def set_wait(s):
        send(sets.at[s], sets.at[s], set_s.at[0], set_r.at[s], (0, me_r)).wait_recv()

    @pl.when(me_s != 1)
    def _():
        set_copy().start()

    def finals(section, lo):
        return [
            send(part, fin.at[me_r], f_s.at[e * R + d], f_r.at[me_r], (section + e, (me_r + d) % R))
            for e in range(lo)
            for d in range(R)
            if e + d
        ]

    setting = lambda s: sets[s, 0:1, :].astype(jnp.int32)

    @pl.when(me_s == 0)
    def _():
        u = stacked(wide[...])

        def piece(d, carry):
            to = (me_r + d) % R
            snd[to] = folded(nt(u, place[pl.ds(pl.multiple_of(to * rows, rows), rows), :]))
            send(snd.at[to], uland.at[me_r], u_s.at[to], u_r.at[me_r], (1, to)).start()
            return carry

        lax.fori_loop(0, R, piece, 0)
        ur, ui = wide[0:P_, :], wide[P_:C2, :]
        pr, pi = probe_ref[0:1, :], probe_ref[1:2, :]
        hit = rows_of((P_, count)) == set_own[0:1, :].astype(jnp.int32)
        re = jnp.sum(ur * pr - ui * pi, axis=1, keepdims=True)
        im = jnp.sum(ur * pi + ui * pr, axis=1, keepdims=True)
        part[...] = jnp.zeros_like(part)
        part[0:1, :] = jnp.sum(jnp.where(hit, re, 0.0), axis=0, keepdims=True)
        part[1:2, :] = jnp.sum(jnp.where(hit, im, 0.0), axis=0, keepdims=True)
        fin[me_r] = part[...]
        for copy in finals(0, 1):
            copy.start()

    @pl.when(me_s == 3)
    def _():
        for d in range(R):
            to = (me_r + d) % R
            send(own, vland.at[me_r], v_s.at[d], v_r.at[me_r], (2, to)).start()

    def w_copy(g, t):
        to = (me_r + 2 * t) % R
        n = wown.shape[0] // GROUPS
        at = pl.ds(pl.multiple_of(g * n, n), n)
        return send(
            wown.at[at], wland.at[me_r // 2, at], w_s.at[g * half + t], w_r.at[(me_r // 2) * GROUPS + g], (1, to)
        )

    def v2_copy(t):
        to = (me_r + 2 * t) % R
        return send(own, v2land.at[me_r // 2], v2_s.at[t], v2_r.at[me_r // 2], (1, to))

    @pl.when(me_s == 2)
    def _():
        for t in range(half):
            v2_copy(t).start()
        for r in range(R):
            send(vland.at[r], vland.at[r], v_s.at[0], v_r.at[r], (3, me_r)).wait_recv()
        y = nn(stacked(vland[0]), place[0:rows, :])
        for r in range(1, R):
            y = y + nn(stacked(vland[r]), place[r * rows : (r + 1) * rows, :])
        hi, lo = y[:C2], y[C2:]
        straight = jnp.concatenate([hi, lo], axis=0).astype(BF16)
        crossed = jnp.concatenate([turned(hi), turned(lo)], axis=0).astype(BF16)

        def group(g, carry):
            for e in range(P_ // GROUPS):
                p = g * (P_ // GROUPS) + e
                z = nt(straight, hl[0, 0, p]) + nt(crossed, hl[1, 0, p])
                z = z + nt(straight, hl[0, 1, p]) + nt(crossed, hl[1, 1, p])
                wown[pl.ds(pl.multiple_of(p * C2, C2), C2), :] = folded(z)
            for t in range(half):
                w_copy(g, t).start()
            return carry

        lax.fori_loop(0, GROUPS, group, 0)

    @pl.when(me_s == 1)
    def _():
        for r in range(R):
            send(uland.at[r], uland.at[r], u_s.at[0], u_r.at[r], (0, me_r)).wait_recv()
        x = uland[0]
        for r in range(1, R):
            x = x + uland[r]
        straight, crossed = stacked(x), stacked(turned(x))

        def front(p, carry):
            z = nn(straight, hl[0, 0, p]) + nn(crossed, hl[1, 0, p])
            z = z + nn(straight, hl[0, 1, p]) + nn(crossed, hl[1, 1, p])
            hi, lo = halves(folded(z))
            at = pl.multiple_of(p * C2, C2)
            bighl[pl.ds(at, C2), :] = hi
            bighl[pl.ds(pl.multiple_of(P_ * C2 + p * C2, C2), C2), :] = lo
            return carry

        lax.fori_loop(0, P_, front, 0)
        n = P_ * C2

        def shuffled(q):
            return folded(nt(bighl[...], place[pl.ds(pl.multiple_of(q * rows, rows), rows), :]))

        def x_copy(t):
            return send(other.at[t], xland.at[t], x_s.at[t], x_r.at[t], (1, partner))

        def give(t, carry):
            other[t] = shuffled(2 * t + 1 - parity)
            x_copy(t).start()
            return carry

        def keep(t, carry):
            mine[t] = shuffled(2 * t + parity)
            return carry

        lax.fori_loop(0, half, give, 0)
        lax.fori_loop(0, half, keep, 0)
        probes = jnp.concatenate([probe_ref[...], jnp.zeros((6, K), F32)], axis=0)
        g1 = folded(nt(stacked(probes), bighl[...]))
        gram[n + C2 : n + C2 + 8, :] = g1[:, :n] + g1[:, n:]
        sets[1] = set_own[...]
        for s in (0, 2, 3):
            set_wait(s)
        hits = [rows_of((n, count)) == setting(1) * C2 + c * P_ + setting(0) for c in range(2)]
        pick = jnp.concatenate([h.astype(F32) for h in hits], axis=1).astype(BF16)

        g2 = jnp.zeros((2 * C2, 2 * n), F32)
        for t in range(half):
            x_copy(t).wait_recv()
            both = mine[t] + xland[t]
            hi, lo = halves(both)
            big[t, 0:n, :] = hi
            big[t, n : 2 * n, :] = lo
            send(v2land.at[t], v2land.at[t], v2_s.at[0], v2_r.at[t], (2, me_r)).wait_recv()
            g2 = g2 + nt(stacked(v2land[t]), big[t])
        g2 = folded(g2)
        gram[n : n + C2, :] = g2[:, :n] + g2[:, n:]

        m = n // GROUPS
        for g in range(GROUPS):
            acc = jnp.zeros((2 * m, 2 * n), F32)
            for t in range(half):
                at = wland.at[t, pl.ds(g * m, m)]
                send(at, at, w_s.at[0], w_r.at[t * GROUPS + g], (2, me_r)).wait_recv()
                acc = acc + nt(stacked(wland[t, g * m : (g + 1) * m, :]), big[t])
            acc = folded(acc)
            gram[g * m : (g + 1) * m, :] = acc[:, :n] + acc[:, n:]

        y = folded(nn(stacked(gram[...]), pick))
        y0, y1 = y[:, :count], y[:, count:]

        def put(row, lo, hi, masks):
            a, b = y0[lo:hi], y1[lo:hi]
            m0, m1 = masks
            part[row : row + 1, :] = jnp.sum(
                jnp.where(m0, a, 0.0) - jnp.where(m1, b, 0.0), axis=0, keepdims=True
            )
            part[row + 1 : row + 2, :] = jnp.sum(
                jnp.where(m1, a, 0.0) + jnp.where(m0, b, 0.0), axis=0, keepdims=True
            )

        part[...] = jnp.zeros_like(part)
        put(0, n + C2, n + C2 + 8, [rows_of((8, count)) == c for c in range(2)])
        put(2, n, n + C2, [rows_of((C2, count)) == c * P_ + setting(2) for c in range(2)])
        put(4, 0, n, [rows_of((n, count)) == setting(2) * C2 + c * P_ + setting(3) for c in range(2)])
        fin[me_r] = part[...]
        for copy in finals(1, S - 1):
            copy.start()
        for t in range(half):
            x_copy(t).wait_send()

    def fin_wait(r):
        send(fin.at[r], fin.at[r], f_s.at[0], f_r.at[r], (1, (me_r + 1) % R)).wait_recv()

    @pl.when(me_s <= 1)
    def _():
        for d in range(1, R):
            fin_wait((me_r + d) % R)

    @pl.when(me_s > 1)
    def _():
        for r in range(R):
            fin_wait(r)

    value = fin[0]
    for r in range(1, R):
        value = value + fin[r]
    total[...] = value
    v = total[...]
    pair = jnp.where(me_s <= 1, v[0:2], jnp.where(me_s == 2, v[2:4], v[4:6]))
    for c in range(2):
        for m in range(micro):
            out_ref[0, c, m : m + 1, :] = pair[c : c + 1, m * batch : (m + 1) * batch]

    @pl.when(me_s != 1)
    def _():
        set_copy().wait_send()

    @pl.when(me_s == 0)
    def _():
        for d in range(R):
            to = (me_r + d) % R
            send(snd.at[to], uland.at[me_r], u_s.at[to], u_r.at[me_r], (1, to)).wait_send()
        for copy in finals(0, 1):
            copy.wait_send()

    @pl.when(me_s == 1)
    def _():
        for copy in finals(1, S - 1):
            copy.wait_send()

    @pl.when(me_s == 2)
    def _():
        for t in range(half):
            v2_copy(t).wait_send()
            for g in range(GROUPS):
                w_copy(g, t).wait_send()

    @pl.when(me_s == 3)
    def _():
        for d in range(R):
            to = (me_r + d) % R
            send(own, vland.at[me_r], v_s.at[d], v_r.at[me_r], (2, to)).wait_send()


def local(bitstrings, boundary, stem_tensor, probe_vectors, inbound_permutations):
    S, R = lax.axis_size("section"), lax.axis_size("stem")
    rows, settings, K = stem_tensor.shape[2:]
    micro, batch, qubits = bitstrings.shape[1:]
    count = micro * batch
    C2 = 2 * settings
    n = settings * C2
    half = R // 2
    dma = pltpu.SemaphoreType.DMA
    scratch = [
        pltpu.VMEM((SLOTS, K // LANES, 2, STEP * settings, LANES), F32),
        pltpu.VMEM((2, 2, settings, rows, K), BF16),
        pltpu.VMEM((K, K), BF16),
        pltpu.VMEM((C2, K), F32),
        pltpu.VMEM((C2, rows), F32),
        pltpu.VMEM((S, 8, count), F32),
        pltpu.VMEM((8, count), F32),
        pltpu.VMEM((R, C2, rows), F32),
        pltpu.VMEM((R, C2, rows), F32),
        pltpu.VMEM((R, C2, rows), F32),
        pltpu.VMEM((half, 2 * n, rows), BF16),
        pltpu.VMEM((2 * n, K), BF16),
        pltpu.VMEM((half, n, rows), F32),
        pltpu.VMEM((half, n, rows), F32),
        pltpu.VMEM((half, n, rows), F32),
        pltpu.VMEM((n, rows), F32),
        pltpu.VMEM((half, n, rows), F32),
        pltpu.VMEM((half, C2, rows), F32),
        pltpu.VMEM((n + C2 + 8, n), F32),
        pltpu.VMEM((8, count), F32),
        pltpu.VMEM((R, 8, count), F32),
        pltpu.VMEM((8, count), F32),
        dma((SLOTS,)),
        dma((1,)),
        dma((S,)),
        dma((R,)),
        dma((R,)),
        dma((R,)),
        dma((R,)),
        dma((half,)),
        dma((half,)),
        dma((half,)),
        dma((half,)),
        dma((GROUPS * half,)),
        dma((GROUPS * half,)),
        dma((S * R,)),
        dma((R,)),
    ]
    out = pl.pallas_call(
        functools.partial(kernel, S, R, rows, settings, K, count),
        out_shape=jax.ShapeDtypeStruct((1, 2, micro, batch), F32),
        in_specs=[VMEM, SMEM, SMEM, VMEM, VMEM, ANY],
        out_specs=VMEM,
        scratch_shapes=scratch,
        compiler_params=pltpu.CompilerParams(
            collective_id=1, has_side_effects=True, vmem_limit_bytes=67_000_000
        ),
    )(
        jnp.transpose(bitstrings[0], (2, 0, 1)),
        boundary,
        inbound_permutations,
        inbound_permutations,
        probe_vectors.reshape(2, K),
        stem_tensor.reshape(2, rows * settings, K),
    )
    return out


def solution(mesh):
    return jax.shard_map(
        local,
        mesh=mesh,
        in_specs=(
            P("section", None, None, None),
            P(),
            P("section", None, "stem", None, None),
            P("section", None, None),
            P(),
        ),
        out_specs=P("section", None, None, None),
        check_vma=False,
    )
```

time: 106 us -> 52.7 us (0.50)
  the two profiles are of different devices: /device:TPU:0 before, /device:TPU:5 now
where the time goes in v1:
time: 52.7 us; the launch traced here: 52.4 us
  Pallas kernels  51.1 us (97%)
  local copies, waits for them, and re-layouts  1.28 us (2%)
    pallas_call x1, Pallas kernels, local(): pl.pallas_call(functools.partial(kernel, S, R, rows, settings, K, count),...  51.1 us
    unnamed x1, local copies, waits for them, and re-layouts  1.28 us

profile of v1, /device:TPU:5, one launch (start us, length us, event | category | flops | bytes accessed | tf_op | source)
XLA Modules:
  0.0 52.4 jit_solution(17039713236855908613)
XLA Ops:
  0.0 51.1 %shard_map.55 = f32[1,2,4,32]{3,2,1,0:T(4,128)} custom-call(s32[3,4,32]{2,1,0:T(4,128)} %bitcast.7, f32[2,2048]{1,0:T(2,128)} %bnd_ref.1, s32[4,2048]{1,0:T(4,128)} %perm_ref.1, s32[4,2048]{1,0:T(4,128)} %perm_ref.1, f32[2,2048]{1,0:T(2,128)} %bitcast.6, f32[2,2048,2048]{2,1,0:T(8,128)} %bitcast.5), custom_call_target="tpu_custom_call" | custom-call | tf_op jit(solution)/shard_map/pallas_call | solution.py:500
  51.1 1.3 %copy.7 = f32[1,2,4,32]{3,2,1,0:T(4,128)} copy(f32[1,2,4,32]{3,2,1,0:T(4,128)} %shard_map.55) | data formatting | bytes 2048

commit v2 on v1

--- a/solution.py
+++ b/solution.py
@@ -9,13 +9,12 @@
 
 MESH = pl.DeviceIdType.MESH
 VMEM = pl.BlockSpec(memory_space=pltpu.VMEM)
-SMEM = pl.BlockSpec(memory_space=pltpu.SMEM)
 ANY = pl.BlockSpec(memory_space=pl.ANY)
 F32, BF16 = jnp.float32, jnp.bfloat16
 LANES = 128
 SLOTS = 4
 STEP = 16
-GROUPS = 4
+VIA = 3
 
 
 def send(src, dst, send_sem, recv_sem, target):
@@ -61,10 +60,11 @@
 
 def kernel(
     S, R, rows, P_, K, count,
-    bits_ref, bnd_ref, perm0_ref, perm_ref, probe_ref, stem_ref, out_ref,
-    buf, hl, place, wide, own, sets, set_own, uland, vland, snd, big, bighl, mine, other, xland, wown, wland, v2land,
-    gram, part, fin, total,
-    load_sem, set_s, set_r, u_s, u_r, v_s, v_r, v2_s, v2_r, x_s, x_r, w_s, w_r, f_s, f_r,
+    bits_hbm, bnd_hbm, perm_hbm, probe_hbm, stem_ref, out_ref,
+    bits_ref, bnd_ref, perm0_ref, perm_ref, probe_ref,
+    buf, hl, place, marks, masks, vecs, tails, wide, own, sets, set_own, uland, vland, snd, big, bighl, mine, other, xland, wown,
+    wland, v2own, v2land, gram, part, fin,
+    small_sem, load_sem, set_s, set_r, u_s, u_r, v_s, v_r, v2_s, v2_r, x_s, x_r, w_s, w_r, f_s, f_r,
 ):
     me_s, me_r = lax.axis_index("section"), lax.axis_index("stem")
     half = R // 2
@@ -86,7 +86,16 @@
     def loaded(slot):
         pltpu.make_async_copy(buf.at[slot], buf.at[slot], load_sem.at[slot]).wait()
 
-    for i in range(min(SLOTS, chunks)):
+    smalls = [
+        pltpu.make_async_copy(src, dst, small_sem.at[e])
+        for e, (src, dst) in enumerate(
+            [(perm_hbm, perm_ref), (probe_hbm, probe_ref), (bits_hbm, bits_ref), (bnd_hbm, bnd_ref), (perm_hbm, perm0_ref)]
+        )
+    ]
+    load(0)
+    for copy in smalls:
+        copy.start()
+    for i in range(1, min(SLOTS, chunks)):
         load(i)
 
     barrier = pltpu.get_barrier_semaphore()
@@ -96,6 +105,11 @@
                 pl.semaphore_signal(
                     barrier, inc=1, device_id=((me_s + e) % S, (me_r + d) % R), device_id_type=MESH
                 )
+
+    own[...] = jnp.zeros_like(own)
+    wide[...] = jnp.zeros_like(wide)
+    for copy in smalls:
+        copy.wait()
 
     qubits, micro, batch = bits_ref.shape
     codes = bits_ref[0].astype(F32)
@@ -107,20 +121,39 @@
         spread = spread + nn(jnp.broadcast_to(codes[m : m + 1, :], (8, batch)).astype(BF16), shift)
     set_own[...] = spread
 
-    own[...] = jnp.zeros_like(own)
-    wide[...] = jnp.zeros_like(wide)
-
     blocks = tiles // chunks
+    parts = 2 if rows % (2 * LANES) == 0 else 1
+
+    def one(hit):
+        return hit.astype(F32).astype(BF16)
+
+    def columns(row):
+        return jnp.broadcast_to(row, (LANES, LANES)).T
+
+    @pl.when(me_s == 0)
+    def _():
+        row = perm_ref[1:2, :]
+        place[0:LANES, :] = one(rows_of((LANES, K)) == row % LANES)
+        marks[...] = jnp.broadcast_to(row // LANES, (2 * C2, K))
+
+    @pl.when(me_s == 2)
+    def _():
+        row = perm_ref[3:4, :]
+        high = jnp.broadcast_to(row // LANES, (2 * C2, K))
+        for a in range(tiles):
+            masks[a * 2 * C2 : (a + 1) * 2 * C2, :] = one(high == a)
+        low = (row % LANES).astype(F32)
+        for b in range(tiles):
+            at = slice(b * LANES, (b + 1) * LANES)
+            place[at, 0:LANES] = one(columns(low[:, at]) == lanes_of((LANES, LANES)).astype(F32))
 
     def build(i):
         for b in range(blocks):
             start = pl.multiple_of((i * blocks + b) * LANES, LANES)
-            every = perm_ref[:, pl.ds(start, LANES)].astype(F32)
-            row = jnp.sum(jnp.where(rows_of((S, LANES)) == (me_s + 1) % S, every, 0.0), axis=0, keepdims=True)
-            col = jnp.broadcast_to(row, (LANES, LANES)).T
+            col = columns(perm_ref[2:3, pl.ds(start, LANES)].astype(F32))
             for j in range(tiles):
                 target = (lanes_of((LANES, LANES)) + j * LANES).astype(F32)
-                place[pl.ds(start, LANES), j * LANES : (j + 1) * LANES] = (col == target).astype(F32).astype(BF16)
+                place[pl.ds(start, LANES), j * LANES : (j + 1) * LANES] = one(col == target)
 
     def first(i, slot):
         scal = []
@@ -179,7 +212,7 @@
 
         lax.fori_loop(0, tiles, column, 0)
 
-    @pl.when(me_s >= 2)
+    @pl.when(me_s == 3)
     def _():
         wide[0:P_, :] = jnp.broadcast_to(probe_ref[0:1, :], (P_, K))
         wide[P_:C2, :] = jnp.broadcast_to(probe_ref[1:2, :], (P_, K))
@@ -190,7 +223,6 @@
 
         @pl.when(me_s == 0)
         def _():
-            build(i)
             first(i, slot)
 
         @pl.when(me_s == 1)
@@ -200,9 +232,7 @@
 
         @pl.when(me_s == 2)
         def _():
-            build(i)
             split(i, slot)
-            against_probe(i, slot)
 
         @pl.when(me_s == 3)
         def _():
@@ -214,8 +244,21 @@
 
         return carry
 
-    lax.fori_loop(0, chunks, stream, 0)
-    pl.semaphore_wait(barrier, S * R - 1)
+    def v_copy(e, d):
+        to = (me_r + d) % R
+        n = rows // parts
+        at = (slice(None), pl.ds(e * n, n))
+        return send(own.at[at], vland.at[(me_r,) + at], v_s.at[e * R + d], v_r.at[me_r * parts + e], (2, to))
+
+    for e in range(parts):
+        lax.fori_loop(e * (chunks // parts), (e + 1) * (chunks // parts), stream, 0)
+        if e == 0:
+            pl.semaphore_wait(barrier, S * R - 1)
+
+        @pl.when(me_s == 3)
+        def _():
+            for d in range(R):
+                v_copy(e, d).start()
 
     def set_copy():
         return send(set_own, sets.at[me_s], set_s.at[0], set_r.at[me_s], (1, me_r))
@@ -240,14 +283,26 @@
     @pl.when(me_s == 0)
     def _():
         u = stacked(wide[...])
-
-        def piece(d, carry):
-            to = (me_r + d) % R
-            snd[to] = folded(nt(u, place[pl.ds(pl.multiple_of(to * rows, rows), rows), :]))
-            send(snd.at[to], uland.at[me_r], u_s.at[to], u_r.at[me_r], (1, to)).start()
-            return carry
-
-        lax.fori_loop(0, R, piece, 0)
+        tall = jnp.concatenate([u[:, a * LANES : (a + 1) * LANES] for a in range(tiles)], axis=0)
+        span = max(rows, LANES)
+
+        def spot(d, carry):
+            step = (me_r * rows // span + d) % (K // span)
+            at = pl.ds(pl.multiple_of(step * span, span), span)
+            z = nn(tails[...], place[0:LANES, at])
+            mark = marks[:, at]
+            got = z[0 : 2 * C2]
+            for a in range(1, tiles):
+                got = jnp.where(mark == a, z[a * 2 * C2 : (a + 1) * 2 * C2], got)
+            got = folded(got)
+            for e in range(span // rows):
+                to = step * (span // rows) + e
+                snd[to] = got[:, e * rows : (e + 1) * rows]
+                send(snd.at[to], uland.at[me_r], u_s.at[to], u_r.at[me_r], (1, to)).start()
+            return carry
+
+        tails[...] = tall
+        lax.fori_loop(0, K // span, spot, 0)
         ur, ui = wide[0:P_, :], wide[P_:C2, :]
         pr, pi = probe_ref[0:1, :], probe_ref[1:2, :]
         hit = rows_of((P_, count)) == set_own[0:1, :].astype(jnp.int32)
@@ -260,48 +315,81 @@
         for copy in finals(0, 1):
             copy.start()
 
-    @pl.when(me_s == 3)
-    def _():
-        for d in range(R):
-            to = (me_r + d) % R
-            send(own, vland.at[me_r], v_s.at[d], v_r.at[me_r], (2, to)).start()
-
-    def w_copy(g, t):
+    def w_copy(p, t):
         to = (me_r + 2 * t) % R
-        n = wown.shape[0] // GROUPS
-        at = pl.ds(pl.multiple_of(g * n, n), n)
+        at = pl.ds(pl.multiple_of(p * C2, C2), C2)
         return send(
-            wown.at[at], wland.at[me_r // 2, at], w_s.at[g * half + t], w_r.at[(me_r // 2) * GROUPS + g], (1, to)
+            wown.at[at], wland.at[me_r // 2, at], w_s.at[p * half + t], w_r.at[(me_r // 2) * P_ + p], (jnp.minimum(p // VIA, 1), to)
         )
 
-    def v2_copy(t):
+    def relay(p, t):
+        at = pl.ds(pl.multiple_of(p * C2, C2), C2)
+        return send(wland.at[t, at], wland.at[t, at], w_s.at[p * half + t], w_r.at[t * P_ + p], (1, me_r))
+
+    def w_wait(p, t):
+        relay(p, t).wait_recv()
+
+    def v2_copy(e, t):
         to = (me_r + 2 * t) % R
-        return send(own, v2land.at[me_r // 2], v2_s.at[t], v2_r.at[me_r // 2], (1, to))
+        at = pl.ds(pl.multiple_of(e * P_, P_), P_)
+        return send(v2own.at[e], v2land.at[me_r // 2, at], v2_s.at[e * half + t], v2_r.at[(me_r // 2) * 2 + e], (1, to))
+
+    @pl.when(me_s == 0)
+    def _():
+        def hop(q, carry):
+            for t in range(half):
+                w_wait(q, t)
+                relay(q, t).start()
+            return carry
+
+        lax.fori_loop(0, VIA, hop, 0)
 
     @pl.when(me_s == 2)
     def _():
-        for t in range(half):
-            v2_copy(t).start()
         for r in range(R):
-            send(vland.at[r], vland.at[r], v_s.at[0], v_r.at[r], (3, me_r)).wait_recv()
-        y = nn(stacked(vland[0]), place[0:rows, :])
-        for r in range(1, R):
-            y = y + nn(stacked(vland[r]), place[r * rows : (r + 1) * rows, :])
+            for e in range(parts):
+                n = rows // parts
+                at = vland.at[r, :, pl.ds(e * n, n)]
+                send(at, at, v_s.at[0], v_r.at[r * parts + e], (3, me_r)).wait_recv()
+        z = None
+        for r in range(R):
+            at = slice(r * rows, (r + 1) * rows)
+            v = stacked(vland[r])
+            tall = jnp.concatenate(
+                [masks[a * 2 * C2 : (a + 1) * 2 * C2, at] * v for a in range(tiles)], axis=0
+            )
+            y = nn(tall, place[at, 0:LANES])
+            z = y if z is None else z + y
+        y = jnp.concatenate([z[a * 2 * C2 : (a + 1) * 2 * C2] for a in range(tiles)], axis=1)
         hi, lo = y[:C2], y[C2:]
-        straight = jnp.concatenate([hi, lo], axis=0).astype(BF16)
-        crossed = jnp.concatenate([turned(hi), turned(lo)], axis=0).astype(BF16)
-
-        def group(g, carry):
-            for e in range(P_ // GROUPS):
-                p = g * (P_ // GROUPS) + e
-                z = nt(straight, hl[0, 0, p]) + nt(crossed, hl[1, 0, p])
-                z = z + nt(straight, hl[0, 1, p]) + nt(crossed, hl[1, 1, p])
-                wown[pl.ds(pl.multiple_of(p * C2, C2), C2), :] = folded(z)
+        probe = probe_ref[...]
+
+        def ends(x):
+            return [h.astype(F32) for h in halves(jnp.concatenate([x] * (P_ // 2), axis=0))]
+
+        straight = jnp.concatenate([hi, lo] + ends(probe), axis=0).astype(BF16)
+        crossed = jnp.concatenate([turned(hi), turned(lo)] + ends(turned(probe)), axis=0).astype(BF16)
+        vecs[0] = straight
+        vecs[1] = crossed
+        v2own[...] = jnp.zeros_like(v2own)
+
+        def back(p, carry):
+            z = nt(vecs[0], hl[0, 0, p]) + nt(vecs[1], hl[1, 0, p])
+            z = z + nt(vecs[0], hl[0, 1, p]) + nt(vecs[1], hl[1, 1, p])
+            wown[pl.ds(pl.multiple_of(p * C2, C2), C2), :] = folded(z[: 2 * C2])
+            e = p // (P_ // 2)
+            v2own[e] = jnp.where(rows_of((P_, rows)) // 2 == p % (P_ // 2), folded(z[2 * C2 :]), v2own[e])
             for t in range(half):
-                w_copy(g, t).start()
-            return carry
-
-        lax.fori_loop(0, GROUPS, group, 0)
+                w_copy(p, t).start()
+
+            @pl.when((p + 1) % (P_ // 2) == 0)
+            def _():
+                for t in range(half):
+                    v2_copy(e, t).start()
+
+            return carry
+
+        lax.fori_loop(0, P_, back, 0)
 
     @pl.when(me_s == 1)
     def _():
@@ -350,27 +438,34 @@
         hits = [rows_of((n, count)) == setting(1) * C2 + c * P_ + setting(0) for c in range(2)]
         pick = jnp.concatenate([h.astype(F32) for h in hits], axis=1).astype(BF16)
 
-        g2 = jnp.zeros((2 * C2, 2 * n), F32)
         for t in range(half):
             x_copy(t).wait_recv()
-            both = mine[t] + xland[t]
-            hi, lo = halves(both)
+            hi, lo = halves(mine[t] + xland[t])
             big[t, 0:n, :] = hi
             big[t, n : 2 * n, :] = lo
-            send(v2land.at[t], v2land.at[t], v2_s.at[0], v2_r.at[t], (2, me_r)).wait_recv()
-            g2 = g2 + nt(stacked(v2land[t]), big[t])
-        g2 = folded(g2)
-        gram[n : n + C2, :] = g2[:, :n] + g2[:, n:]
-
-        m = n // GROUPS
-        for g in range(GROUPS):
-            acc = jnp.zeros((2 * m, 2 * n), F32)
+
+        def inner(q, carry):
+            p = q
+            at = pl.ds(pl.multiple_of(p * C2, C2), C2)
             for t in range(half):
-                at = wland.at[t, pl.ds(g * m, m)]
-                send(at, at, w_s.at[0], w_r.at[t * GROUPS + g], (2, me_r)).wait_recv()
-                acc = acc + nt(stacked(wland[t, g * m : (g + 1) * m, :]), big[t])
+                w_wait(p, t)
+            acc = nt(stacked(wland[0, at, :]), big[0])
+            for t in range(1, half):
+                acc = acc + nt(stacked(wland[t, at, :]), big[t])
             acc = folded(acc)
-            gram[g * m : (g + 1) * m, :] = acc[:, :n] + acc[:, n:]
+            gram[at, :] = acc[:, :n] + acc[:, n:]
+            return carry
+
+        lax.fori_loop(0, P_, inner, 0)
+        acc = None
+        for t in range(half):
+            for e in range(2):
+                at = v2land.at[t, pl.ds(e * P_, P_)]
+                send(at, at, v2_s.at[0], v2_r.at[t * 2 + e], (2, me_r)).wait_recv()
+            got = nt(stacked(v2land[t]), big[t])
+            acc = got if acc is None else acc + got
+        acc = folded(acc)
+        gram[n : n + C2, :] = acc[:, :n] + acc[:, n:]
 
         y = folded(nn(stacked(gram[...]), pick))
         y0, y1 = y[:, :count], y[:, count:]
@@ -387,7 +482,7 @@
 
         part[...] = jnp.zeros_like(part)
         put(0, n + C2, n + C2 + 8, [rows_of((8, count)) == c for c in range(2)])
-        put(2, n, n + C2, [rows_of((C2, count)) == c * P_ + setting(2) for c in range(2)])
+        put(2, n, n + C2, [rows_of((C2, count)) == setting(2) * 2 + c for c in range(2)])
         put(4, 0, n, [rows_of((n, count)) == setting(2) * C2 + c * P_ + setting(3) for c in range(2)])
         fin[me_r] = part[...]
         for copy in finals(1, S - 1):
@@ -411,8 +506,7 @@
     value = fin[0]
     for r in range(1, R):
         value = value + fin[r]
-    total[...] = value
-    v = total[...]
+    v = value
     pair = jnp.where(me_s <= 1, v[0:2], jnp.where(me_s == 2, v[2:4], v[4:6]))
     for c in range(2):
         for m in range(micro):
@@ -429,6 +523,9 @@
             send(snd.at[to], uland.at[me_r], u_s.at[to], u_r.at[me_r], (1, to)).wait_send()
         for copy in finals(0, 1):
             copy.wait_send()
+        for p in range(VIA):
+            for t in range(half):
+                relay(p, t).wait_send()
 
     @pl.when(me_s == 1)
     def _():
@@ -438,15 +535,16 @@
     @pl.when(me_s == 2)
     def _():
         for t in range(half):
-            v2_copy(t).wait_send()
-            for g in range(GROUPS):
-                w_copy(g, t).wait_send()
+            for e in range(2):
+                v2_copy(e, t).wait_send()
+            for p in range(P_):
+                w_copy(p, t).wait_send()
 
     @pl.when(me_s == 3)
     def _():
-        for d in range(R):
-            to = (me_r + d) % R
-            send(own, vland.at[me_r], v_s.at[d], v_r.at[me_r], (2, to)).wait_send()
+        for e in range(parts):
+            for d in range(R):
+                v_copy(e, d).wait_send()
 
 
 def local(bitstrings, boundary, stem_tensor, probe_vectors, inbound_permutations):
@@ -459,9 +557,18 @@
     half = R // 2
     dma = pltpu.SemaphoreType.DMA
     scratch = [
+        pltpu.VMEM((qubits, micro, batch), jnp.int32),
+        pltpu.SMEM(boundary.shape, F32),
+        pltpu.SMEM(inbound_permutations.shape, jnp.int32),
+        pltpu.VMEM(inbound_permutations.shape, jnp.int32),
+        pltpu.VMEM((2, K), F32),
         pltpu.VMEM((SLOTS, K // LANES, 2, STEP * settings, LANES), F32),
         pltpu.VMEM((2, 2, settings, rows, K), BF16),
         pltpu.VMEM((K, K), BF16),
+        pltpu.VMEM((2 * C2, K), jnp.int32),
+        pltpu.VMEM((2 * C2 * (K // LANES), K), BF16),
+        pltpu.VMEM((2, 3 * C2, K), BF16),
+        pltpu.VMEM((2 * C2 * (K // LANES), LANES), BF16),
         pltpu.VMEM((C2, K), F32),
         pltpu.VMEM((C2, rows), F32),
         pltpu.VMEM((S, 8, count), F32),
@@ -476,31 +583,32 @@
         pltpu.VMEM((half, n, rows), F32),
         pltpu.VMEM((n, rows), F32),
         pltpu.VMEM((half, n, rows), F32),
+        pltpu.VMEM((2, settings, rows), F32),
         pltpu.VMEM((half, C2, rows), F32),
         pltpu.VMEM((n + C2 + 8, n), F32),
         pltpu.VMEM((8, count), F32),
         pltpu.VMEM((R, 8, count), F32),
-        pltpu.VMEM((8, count), F32),
+        dma((5,)),
         dma((SLOTS,)),
         dma((1,)),
         dma((S,)),
         dma((R,)),
         dma((R,)),
-        dma((R,)),
-        dma((R,)),
+        dma((2 * R,)),
+        dma((2 * R,)),
+        dma((2 * half,)),
+        dma((2 * half,)),
         dma((half,)),
         dma((half,)),
-        dma((half,)),
-        dma((half,)),
-        dma((GROUPS * half,)),
-        dma((GROUPS * half,)),
+        dma((settings * half,)),
+        dma((settings * half,)),
         dma((S * R,)),
         dma((R,)),
     ]
     out = pl.pallas_call(
         functools.partial(kernel, S, R, rows, settings, K, count),
         out_shape=jax.ShapeDtypeStruct((1, 2, micro, batch), F32),
-        in_specs=[VMEM, SMEM, SMEM, VMEM, VMEM, ANY],
+        in_specs=[ANY] * 5,
         out_specs=VMEM,
         scratch_shapes=scratch,
         compiler_params=pltpu.CompilerParams(
@@ -509,7 +617,6 @@
     )(
         jnp.transpose(bitstrings[0], (2, 0, 1)),
         boundary,
-        inbound_permutations,
         inbound_permutations,
         probe_vectors.reshape(2, K),
         stem_tensor.reshape(2, rows * settings, K),

time: 52.7 us -> 45.9 us (0.87)
  Pallas kernels: 51.1 us -> 44.5 us
    pallas_call x1, Pallas kernels: 51.1 us -> 44.5 us  [local(): pl.pallas_call(functools.partial(kernel, S, R, rows, settings, K, count),...]
where the time goes in v2:
time: 45.9 us; the launch traced here: 45.7 us
  Pallas kernels  44.5 us (97%)
  local copies, waits for them, and re-layouts  1.28 us (3%)
    pallas_call x1, Pallas kernels, local(): pl.pallas_call(functools.partial(kernel, S, R, rows, settings, K, count),...  44.5 us
    unnamed x1, local copies, waits for them, and re-layouts  1.28 us

profile of v2, /device:TPU:5, one launch (start us, length us, event | category | flops | bytes accessed | tf_op | source)
XLA Modules:
  0.0 45.7 jit_solution(10174290707258951860)
XLA Ops:
  0.0 44.5 %shard_map.55 = f32[1,2,4,32]{3,2,1,0:T(4,128)} custom-call(s32[3,4,32]{2,1,0:T(4,128)} %bitcast.7, f32[2,2048]{1,0:T(2,128)} %bnd_hbm.1, s32[4,2048]{1,0:T(4,128)} %perm_hbm.1, f32[2,2048]{1,0:T(2,128)} %bitcast.6, f32[2,2048,2048]{2,1,0:T(8,128)} %bitcast.5), custom_call_target="tpu_custom_call" | custom-call | tf_op jit(solution)/shard_map/pallas_call | solution.py:608
  44.5 1.3 %copy.7 = f32[1,2,4,32]{3,2,1,0:T(4,128)} copy(f32[1,2,4,32]{3,2,1,0:T(4,128)} %shard_map.55) | data formatting | bytes 2048

commit v3 on v2

--- a/solution.py
+++ b/solution.py
@@ -14,7 +14,7 @@
 LANES = 128
 SLOTS = 4
 STEP = 16
-VIA = 3
+BLOCK = 256
 
 
 def send(src, dst, send_sem, recv_sem, target):
@@ -58,11 +58,18 @@
     return lax.broadcasted_iota(jnp.int32, shape, 1)
 
 
-def kernel(
+def kernel(shared, S, R, rows, P_, K, count, *refs):
+    refs = list(refs)
+    if shared:
+        refs.insert(13, refs[12])
+    body(S, R, rows, P_, K, count, *refs)
+
+
+def body(
     S, R, rows, P_, K, count,
     bits_hbm, bnd_hbm, perm_hbm, probe_hbm, stem_ref, out_ref,
     bits_ref, bnd_ref, perm0_ref, perm_ref, probe_ref,
-    buf, hl, place, marks, masks, vecs, tails, wide, own, sets, set_own, uland, vland, snd, big, bighl, mine, other, xland, wown,
+    buf, hl, hlt, place, marks, masks, vecs, tails, wide, own, sets, set_own, uland, vland, snd, big, bighl, mine, other, xland, wown,
     wland, v2own, v2land, gram, part, fin,
     small_sem, load_sem, set_s, set_r, u_s, u_r, v_s, v_r, v2_s, v2_r, x_s, x_r, w_s, w_r, f_s, f_r,
 ):
@@ -74,11 +81,23 @@
     C2 = 2 * P_
     tiles = K // LANES
 
+    block = min(rows, LANES)
+    deep = block // STEP
+    broad = tiles // deep
+    across = tiles // broad
+    turning = me_s == 2
+
     def load(i):
         slot = i % SLOTS
         for j in range(tiles):
+            row = jnp.where(turning, (i // across) * deep + j // broad, i)
+            col = jnp.where(turning, (i % across) * broad + j % broad, j)
             pltpu.make_async_copy(
-                stem_ref.at[:, pl.ds(i * STEP * P_, STEP * P_), pl.ds(j * LANES, LANES)],
+                stem_ref.at[
+                    :,
+                    pl.ds(pl.multiple_of(row * STEP * P_, STEP * P_), STEP * P_),
+                    pl.ds(pl.multiple_of(col * LANES, LANES), LANES),
+                ],
                 buf.at[slot, j],
                 load_sem.at[slot],
             ).start()
@@ -202,15 +221,31 @@
         at = pl.ds(pl.multiple_of(i * STEP, STEP), STEP)
 
         def column(j, carry):
-            js = pl.ds(pl.multiple_of(j * LANES, LANES), LANES)
+            js = pl.ds(pl.multiple_of(j % (BLOCK // LANES) * LANES, LANES), LANES)
             for c in range(2):
                 for p in range(P_):
                     hi, lo = halves(buf[slot, j, c, pl.ds(p, STEP, P_), :])
-                    hl[c, 0, p, at, js] = hi
-                    hl[c, 1, p, at, js] = lo
+                    hl[c, 0, p, j // (BLOCK // LANES), at, js] = hi
+                    hl[c, 1, p, j // (BLOCK // LANES), at, js] = lo
             return carry
 
         lax.fori_loop(0, tiles, column, 0)
+
+    def split_turned(i, slot):
+        at = pl.ds(pl.multiple_of(i // across * block, block), block) if rows > block else slice(None)
+
+        def column(e, carry):
+            j, c = e // 2, e % 2
+            tile = (i % across) * broad + j
+            js = pl.ds(pl.multiple_of(tile % (BLOCK // LANES) * LANES, LANES), LANES)
+            for p in range(P_):
+                x = [buf[slot, d * broad + j, c, pl.ds(p, STEP, P_), :] for d in range(deep)]
+                hi, lo = halves(jnp.concatenate(x, axis=0).T)
+                hlt[c, 0, p, tile // (BLOCK // LANES), js, at] = hi
+                hlt[c, 1, p, tile // (BLOCK // LANES), js, at] = lo
+            return carry
+
+        lax.fori_loop(0, 2 * broad, column, 0)
 
     @pl.when(me_s == 3)
     def _():
@@ -232,7 +267,7 @@
 
         @pl.when(me_s == 2)
         def _():
-            split(i, slot)
+            split_turned(i, slot)
 
         @pl.when(me_s == 3)
         def _():
@@ -272,7 +307,7 @@
 
     def finals(section, lo):
         return [
-            send(part, fin.at[me_r], f_s.at[e * R + d], f_r.at[me_r], (section + e, (me_r + d) % R))
+            send(part.at[e], fin.at[me_r], f_s.at[e * R + d], f_r.at[me_r], (section + e, (me_r + d) % R))
             for e in range(lo)
             for d in range(R)
             if e + d
@@ -308,26 +343,34 @@
         hit = rows_of((P_, count)) == set_own[0:1, :].astype(jnp.int32)
         re = jnp.sum(ur * pr - ui * pi, axis=1, keepdims=True)
         im = jnp.sum(ur * pi + ui * pr, axis=1, keepdims=True)
-        part[...] = jnp.zeros_like(part)
-        part[0:1, :] = jnp.sum(jnp.where(hit, re, 0.0), axis=0, keepdims=True)
-        part[1:2, :] = jnp.sum(jnp.where(hit, im, 0.0), axis=0, keepdims=True)
-        fin[me_r] = part[...]
+        part[0, 0:1, :] = jnp.sum(jnp.where(hit, re, 0.0), axis=0, keepdims=True)
+        part[0, 1:2, :] = jnp.sum(jnp.where(hit, im, 0.0), axis=0, keepdims=True)
+        fin[me_r] = part[0]
         for copy in finals(0, 1):
             copy.start()
 
+    mid = P_ // 2
+    relayed = [q + q // (mid - 1) for q in range(mid)]
+    spot = me_r // 2
+
+    def w_rows(p):
+        return pl.ds(pl.multiple_of(p * C2, C2), C2)
+
     def w_copy(p, t):
-        to = (me_r + 2 * t) % R
-        at = pl.ds(pl.multiple_of(p * C2, C2), C2)
-        return send(
-            wown.at[at], wland.at[me_r // 2, at], w_s.at[p * half + t], w_r.at[(me_r // 2) * P_ + p], (jnp.minimum(p // VIA, 1), to)
-        )
+        at, to = w_rows(p), (me_r + 2 * t) % R
+        return send(wown.at[at], wland.at[spot, at], w_s.at[p * half + t], w_r.at[spot * P_ + p], (1, to))
+
+    def w_lend(p):
+        at = w_rows(p)
+        return send(wown.at[at], wland.at[spot, at], w_s.at[p * half], w_r.at[spot * P_ + p], (0, me_r))
 
     def relay(p, t):
-        at = pl.ds(pl.multiple_of(p * C2, C2), C2)
-        return send(wland.at[t, at], wland.at[t, at], w_s.at[p * half + t], w_r.at[t * P_ + p], (1, me_r))
+        at, to = (spot, w_rows(p)), (me_r + 2 * t) % R
+        return send(wland.at[at], wland.at[at], w_s.at[p * half + t], w_r.at[spot * P_ + p], (1, to))
 
     def w_wait(p, t):
-        relay(p, t).wait_recv()
+        at = (t, w_rows(p))
+        send(wland.at[at], wland.at[at], w_s.at[p * half], w_r.at[t * P_ + p], (2, me_r)).wait_recv()
 
     def v2_copy(e, t):
         to = (me_r + 2 * t) % R
@@ -337,12 +380,13 @@
     @pl.when(me_s == 0)
     def _():
         def hop(q, carry):
+            p = q + q // (mid - 1)
+            w_wait(p, spot)
             for t in range(half):
-                w_wait(q, t)
-                relay(q, t).start()
-            return carry
-
-        lax.fori_loop(0, VIA, hop, 0)
+                relay(p, t).start()
+            return carry
+
+        lax.fori_loop(0, mid, hop, 0)
 
     @pl.when(me_s == 2)
     def _():
@@ -373,23 +417,40 @@
         vecs[1] = crossed
         v2own[...] = jnp.zeros_like(v2own)
 
-        def back(p, carry):
-            z = nt(vecs[0], hl[0, 0, p]) + nt(vecs[1], hl[1, 0, p])
-            z = z + nt(vecs[0], hl[0, 1, p]) + nt(vecs[1], hl[1, 1, p])
-            wown[pl.ds(pl.multiple_of(p * C2, C2), C2), :] = folded(z[: 2 * C2])
-            e = p // (P_ // 2)
-            v2own[e] = jnp.where(rows_of((P_, rows)) // 2 == p % (P_ // 2), folded(z[2 * C2 :]), v2own[e])
-            for t in range(half):
-                w_copy(p, t).start()
-
-            @pl.when((p + 1) % (P_ // 2) == 0)
+        def back(pair, carry):
+            for odd in range(2):
+                p = 2 * pair + odd
+                z = None
+                for c in range(2):
+                    for h in range(2):
+                        for b in range(K // BLOCK):
+                            y = nn(vecs[c, :, b * BLOCK : (b + 1) * BLOCK], hlt[c, h, p, b])
+                            z = y if z is None else z + y
+                wown[pl.ds(pl.multiple_of(p * C2, C2), C2), :] = folded(z[: 2 * C2])
+                e = p // (P_ // 2)
+                v2own[e] = jnp.where(rows_of((P_, rows)) // 2 == p % (P_ // 2), folded(z[2 * C2 :]), v2own[e])
+
+            @pl.when((pair + 1) % (P_ // 4) == 0)
             def _():
                 for t in range(half):
-                    v2_copy(e, t).start()
-
-            return carry
-
-        lax.fori_loop(0, P_, back, 0)
+                    v2_copy(pair // (P_ // 4), t).start()
+
+            for odd in range(2):
+                p = 2 * pair + odd
+                lent = jnp.logical_or(p < mid - 1, p == mid)
+
+                @pl.when(lent)
+                def _():
+                    w_lend(p).start()
+
+                @pl.when(jnp.logical_not(lent))
+                def _():
+                    for t in range(half):
+                        w_copy(p, t).start()
+
+            return carry
+
+        lax.fori_loop(0, P_ // 2, back, 0)
 
     @pl.when(me_s == 1)
     def _():
@@ -401,12 +462,13 @@
         straight, crossed = stacked(x), stacked(turned(x))
 
         def front(p, carry):
-            z = nn(straight, hl[0, 0, p]) + nn(crossed, hl[1, 0, p])
-            z = z + nn(straight, hl[0, 1, p]) + nn(crossed, hl[1, 1, p])
-            hi, lo = halves(folded(z))
-            at = pl.multiple_of(p * C2, C2)
-            bighl[pl.ds(at, C2), :] = hi
-            bighl[pl.ds(pl.multiple_of(P_ * C2 + p * C2, C2), C2), :] = lo
+            for b in range(K // BLOCK):
+                z = nn(straight, hl[0, 0, p, b]) + nn(crossed, hl[1, 0, p, b])
+                z = z + nn(straight, hl[0, 1, p, b]) + nn(crossed, hl[1, 1, p, b])
+                hi, lo = halves(folded(z))
+                js = slice(b * BLOCK, (b + 1) * BLOCK)
+                bighl[pl.ds(pl.multiple_of(p * C2, C2), C2), js] = hi
+                bighl[pl.ds(pl.multiple_of(P_ * C2 + p * C2, C2), C2), js] = lo
             return carry
 
         lax.fori_loop(0, P_, front, 0)
@@ -445,7 +507,7 @@
             big[t, n : 2 * n, :] = lo
 
         def inner(q, carry):
-            p = q
+            p = q + q // mid - mid * (q // (P_ - 1))
             at = pl.ds(pl.multiple_of(p * C2, C2), C2)
             for t in range(half):
                 w_wait(p, t)
@@ -456,7 +518,7 @@
             gram[at, :] = acc[:, :n] + acc[:, n:]
             return carry
 
-        lax.fori_loop(0, P_, inner, 0)
+        lax.fori_loop(0, P_ - 1, inner, 0)
         acc = None
         for t in range(half):
             for e in range(2):
@@ -466,6 +528,7 @@
             acc = got if acc is None else acc + got
         acc = folded(acc)
         gram[n : n + C2, :] = acc[:, :n] + acc[:, n:]
+        lax.fori_loop(P_ - 1, P_, inner, 0)
 
         y = folded(nn(stacked(gram[...]), pick))
         y0, y1 = y[:, :count], y[:, count:]
@@ -473,18 +536,17 @@
         def put(row, lo, hi, masks):
             a, b = y0[lo:hi], y1[lo:hi]
             m0, m1 = masks
-            part[row : row + 1, :] = jnp.sum(
+            part[row, 0:1, :] = jnp.sum(
                 jnp.where(m0, a, 0.0) - jnp.where(m1, b, 0.0), axis=0, keepdims=True
             )
-            part[row + 1 : row + 2, :] = jnp.sum(
+            part[row, 1:2, :] = jnp.sum(
                 jnp.where(m1, a, 0.0) + jnp.where(m0, b, 0.0), axis=0, keepdims=True
             )
 
-        part[...] = jnp.zeros_like(part)
         put(0, n + C2, n + C2 + 8, [rows_of((8, count)) == c for c in range(2)])
-        put(2, n, n + C2, [rows_of((C2, count)) == setting(2) * 2 + c for c in range(2)])
-        put(4, 0, n, [rows_of((n, count)) == setting(2) * C2 + c * P_ + setting(3) for c in range(2)])
-        fin[me_r] = part[...]
+        put(1, n, n + C2, [rows_of((C2, count)) == setting(2) * 2 + c for c in range(2)])
+        put(2, 0, n, [rows_of((n, count)) == setting(2) * C2 + c * P_ + setting(3) for c in range(2)])
+        fin[me_r] = part[0]
         for copy in finals(1, S - 1):
             copy.start()
         for t in range(half):
@@ -506,11 +568,9 @@
     value = fin[0]
     for r in range(1, R):
         value = value + fin[r]
-    v = value
-    pair = jnp.where(me_s <= 1, v[0:2], jnp.where(me_s == 2, v[2:4], v[4:6]))
     for c in range(2):
         for m in range(micro):
-            out_ref[0, c, m : m + 1, :] = pair[c : c + 1, m * batch : (m + 1) * batch]
+            out_ref[0, c, m : m + 1, :] = value[c : c + 1, m * batch : (m + 1) * batch]
 
     @pl.when(me_s != 1)
     def _():
@@ -523,7 +583,7 @@
             send(snd.at[to], uland.at[me_r], u_s.at[to], u_r.at[me_r], (1, to)).wait_send()
         for copy in finals(0, 1):
             copy.wait_send()
-        for p in range(VIA):
+        for p in relayed:
             for t in range(half):
                 relay(p, t).wait_send()
 
@@ -538,7 +598,10 @@
             for e in range(2):
                 v2_copy(e, t).wait_send()
             for p in range(P_):
-                w_copy(p, t).wait_send()
+                if p not in relayed:
+                    w_copy(p, t).wait_send()
+        for p in relayed:
+            w_lend(p).wait_send()
 
     @pl.when(me_s == 3)
     def _():
@@ -563,7 +626,8 @@
         pltpu.VMEM(inbound_permutations.shape, jnp.int32),
         pltpu.VMEM((2, K), F32),
         pltpu.VMEM((SLOTS, K // LANES, 2, STEP * settings, LANES), F32),
-        pltpu.VMEM((2, 2, settings, rows, K), BF16),
+        pltpu.VMEM((2, 2, settings, K // BLOCK, rows, BLOCK), BF16),
+        pltpu.VMEM((2, 2, settings, K // BLOCK, BLOCK, rows), BF16),
         pltpu.VMEM((K, K), BF16),
         pltpu.VMEM((2 * C2, K), jnp.int32),
         pltpu.VMEM((2 * C2 * (K // LANES), K), BF16),
@@ -586,8 +650,8 @@
         pltpu.VMEM((2, settings, rows), F32),
         pltpu.VMEM((half, C2, rows), F32),
         pltpu.VMEM((n + C2 + 8, n), F32),
-        pltpu.VMEM((8, count), F32),
-        pltpu.VMEM((R, 8, count), F32),
+        pltpu.VMEM((S - 1, 2, count), F32),
+        pltpu.VMEM((R, 2, count), F32),
         dma((5,)),
         dma((SLOTS,)),
         dma((1,)),
@@ -605,8 +669,11 @@
         dma((S * R,)),
         dma((R,)),
     ]
+    shared = rows == BLOCK
+    if shared:
+        scratch.pop(7)
     out = pl.pallas_call(
-        functools.partial(kernel, S, R, rows, settings, K, count),
+        functools.partial(kernel, shared, S, R, rows, settings, K, count),
         out_shape=jax.ShapeDtypeStruct((1, 2, micro, batch), F32),
         in_specs=[ANY] * 5,
         out_specs=VMEM,

time: 45.9 us -> 42.2 us (0.919)
  Pallas kernels: 44.5 us -> 40.8 us
    pallas_call x1, Pallas kernels: 44.5 us -> 40.8 us  [local(): pl.pallas_call(functools.partial(kernel, shared, S, R, rows, settings, K,...]
where the time goes in v3:
time: 42.2 us; the launch traced here: 42 us
  Pallas kernels  40.8 us (97%)
  local copies, waits for them, and re-layouts  1.28 us (3%)
    pallas_call x1, Pallas kernels, local(): pl.pallas_call(functools.partial(kernel, shared, S, R, rows, settings, K,...  40.8 us
    unnamed x1, local copies, waits for them, and re-layouts  1.28 us

profile of v3, /device:TPU:5, one launch (start us, length us, event | category | flops | bytes accessed | tf_op | source)
XLA Modules:
  0.0 42.0 jit_solution(18353730208912818693)
XLA Ops:
  0.0 40.8 %shard_map.55 = f32[1,2,4,32]{3,2,1,0:T(4,128)} custom-call(s32[3,4,32]{2,1,0:T(4,128)} %bitcast.7, f32[2,2048]{1,0:T(2,128)} %refs_1_.1, s32[4,2048]{1,0:T(4,128)} %refs_2_.1, f32[2,2048]{1,0:T(2,128)} %bitcast.6, f32[2,2048,2048]{2,1,0:T(8,128)} %bitcast.5), custom_call_target="tpu_custom_call" | custom-call | tf_op jit(solution)/shard_map/pallas_call | solution.py:675
  40.8 1.3 %copy.7 = f32[1,2,4,32]{3,2,1,0:T(4,128)} copy(f32[1,2,4,32]{3,2,1,0:T(4,128)} %shard_map.55) | data formatting | bytes 2048

commit v4 on v3

--- a/solution.py
+++ b/solution.py
@@ -507,7 +507,7 @@
             big[t, n : 2 * n, :] = lo
 
         def inner(q, carry):
-            p = q + q // mid - mid * (q // (P_ - 1))
+            p = q
             at = pl.ds(pl.multiple_of(p * C2, C2), C2)
             for t in range(half):
                 w_wait(p, t)
@@ -674,7 +674,7 @@
         scratch.pop(7)
     out = pl.pallas_call(
         functools.partial(kernel, shared, S, R, rows, settings, K, count),
-        out_shape=jax.ShapeDtypeStruct((1, 2, micro, batch), F32),
+        out_shape=pltpu.VMEM((1, 2, micro, batch), F32),
         in_specs=[ANY] * 5,
         out_specs=VMEM,
         scratch_shapes=scratch,

time: 42.2 us -> 40.4 us (0.957)
  Pallas kernels: 40.8 us -> 39.7 us
  local copies, waits for them, and re-layouts: 1.28 us -> 0.6 us
    pallas_call x1, Pallas kernels: 40.8 us -> 39.7 us  [local(): pl.pallas_call(functools.partial(kernel, shared, S, R, rows, settings, K,...]
    unnamed x1, local copies, waits for them, and re-layouts: 1.28 us -> 0.6 us
where the time goes in v4:
time: 40.4 us; the launch traced here: 40.3 us
  Pallas kernels  39.7 us (98%)
  local copies, waits for them, and re-layouts  0.6 us (1%)
    pallas_call x1, Pallas kernels, local(): pl.pallas_call(functools.partial(kernel, shared, S, R, rows, settings, K,...  39.7 us

profile of v4, /device:TPU:5, one launch (start us, length us, event | category | flops | bytes accessed | tf_op | source)
XLA Modules:
  0.0 40.3 jit_solution(5625217317312450624)
XLA Ops:
  0.0 39.7 %shard_map.55 = f32[1,2,4,32]{3,2,1,0:T(4,128)S(1)} custom-call(s32[3,4,32]{2,1,0:T(4,128)} %bitcast.7, f32[2,2048]{1,0:T(2,128)} %refs_1_.1, s32[4,2048]{1,0:T(4,128)} %refs_2_.1, f32[2,2048]{1,0:T(2,128)} %bitcast.6, f32[2,2048,2048]{2,1,0:T(8,128)} %bitcast.5), custom_call_target="tpu_custom_call" | custom-call | tf_op jit(solution)/shard_map/pallas_call | solution.py:675
  39.7 0.6 %copy.7 = f32[1,2,4,32]{3,2,1,0:T(4,128)} copy(f32[1,2,4,32]{3,2,1,0:T(4,128)S(1)} %shard_map.55) | data formatting | bytes 2048

commit v5 on v4

--- a/solution.py
+++ b/solution.py
@@ -12,7 +12,7 @@
 ANY = pl.BlockSpec(memory_space=pl.ANY)
 F32, BF16 = jnp.float32, jnp.bfloat16
 LANES = 128
-SLOTS = 4
+SLOTS = 5
 STEP = 16
 BLOCK = 256
 

time: 40.4 us -> 40.3 us (level)
  no operation moved by 1% of the time
where the time goes in v5:
time: 40.3 us; the launch traced here: 40.2 us
  Pallas kernels  39.6 us (98%)
  local copies, waits for them, and re-layouts  0.6 us (1%)
    pallas_call x1, Pallas kernels, local(): pl.pallas_call(functools.partial(kernel, shared, S, R, rows, settings, K,...  39.6 us

profile of v5, /device:TPU:5, one launch (start us, length us, event | category | flops | bytes accessed | tf_op | source)
XLA Modules:
  0.0 40.2 jit_solution(16439856569769313077)
XLA Ops:
  0.0 39.6 %shard_map.55 = f32[1,2,4,32]{3,2,1,0:T(4,128)S(1)} custom-call(s32[3,4,32]{2,1,0:T(4,128)} %bitcast.7, f32[2,2048]{1,0:T(2,128)} %refs_1_.1, s32[4,2048]{1,0:T(4,128)} %refs_2_.1, f32[2,2048]{1,0:T(2,128)} %bitcast.6, f32[2,2048,2048]{2,1,0:T(8,128)} %bitcast.5), custom_call_target="tpu_custom_call" | custom-call | tf_op jit(solution)/shard_map/pallas_call | solution.py:675
  39.6 0.6 %copy.7 = f32[1,2,4,32]{3,2,1,0:T(4,128)} copy(f32[1,2,4,32]{3,2,1,0:T(4,128)S(1)} %shard_map.55) | data formatting | bytes 2048
